TPU v7x, 32 devices: a whole 2x2x4 slice. The times are simulated.
32 devices in a mesh: rows: 8 (over z, x), grp: 4 (over y, core).
Axes of the slice: x: 2, y: 2, z: 4, core: 2. Of those that a mesh axis runs over, the one named last changes fastest.
Arguments:
- visibilities: float32 [2, 131072], P(None, ('rows', 'grp')), may hold values from -6 to 6
- uv_tiles: int32 [2, 131072], P(None, ('rows', 'grp')), may hold values from 0 to 511, as said below
- kernel_offsets: int32 [2, 131072], P(None, ('rows', 'grp')), may hold values from 0 to 7
- kernel: float32 [8, 8], replicated, may hold values from 0.5 to 1.5
Outputs:
- dirty_image: float32 [2, 4096, 4096], P(None, ('rows', 'grp'))
Inputs may be any that keep to these rules, and one draw needn't show every extreme that they name: `uv_tiles`: row 0 holds tile rows, row 1 tile columns. The visibilities of baseline block q (positions q * 4096 to (q + 1) * 4096 - 1), with s = q divided by the number of devices of grp, have tile rows from s * 64 to (s + 1) * 64 - 1.
All inputs are finite; a program needn't handle non-finite values.
Results may differ from a plain program's by a relative error of at most 0.0044.
Values sent between devices are 32-bit elements; how exact they have to be, the bound alone decides.
A program may use at most 128 MiB of HBM per device.

v0:
```python
import math

import jax
import jax.numpy as jnp
from jax import lax
from jax.sharding import PartitionSpec as P

G = 4096


vis_block = 256


def passed_along(x, axis, by):
    peers = lax.axis_size(axis)
    return lax.ppermute(x, axis, [(i, (i + by) % peers) for i in range(peers)])


def phase_table(first_count, second_count, length):
    first_ids = lax.broadcasted_iota(jnp.int32, (first_count, second_count), 0)
    second_ids = lax.broadcasted_iota(jnp.int32, (first_count, second_count), 1)
    angles = (first_ids * second_ids % length).astype(jnp.float32) * (2.0 * math.pi / length)
    return (jnp.cos(angles), jnp.sin(angles))


def complex_einsum(pattern, left_pair, right_pair):

    def product(left_one, right_one):
        return jnp.einsum(pattern, left_one, right_one, precision=lax.Precision.HIGHEST)

    real_out = product(left_pair[0], right_pair[0]) - product(left_pair[1], right_pair[1])
    imag_out = product(left_pair[0], right_pair[1]) + product(left_pair[1], right_pair[0])
    return (real_out, imag_out)


def complex_scale(operand, factor):
    return (
        operand[0] * factor[0] - operand[1] * factor[1],
        operand[0] * factor[1] + operand[1] * factor[0],
    )


def grid_window(visibilities, uv_tiles, kernel_offsets, kernel, row_list, grid_side, block_size):
    vis_count = visibilities.shape[1]
    tap_count = kernel.shape[0]
    window_rows = row_list.shape[0]
    tap_ids = lax.broadcasted_iota(jnp.int32, (1, tap_count), 1)
    row_ids = jnp.broadcast_to(row_list[None, :], (block_size, window_rows))
    col_ids = lax.broadcasted_iota(jnp.int32, (block_size, grid_side), 1)

    def lookup(offsets):
        one_hot = (offsets[:, None] == tap_ids).astype(jnp.float32)
        return jnp.dot(one_hot, kernel, precision=lax.Precision.HIGHEST)

    def add_block(block_index, accumulated):
        block_start = block_index * block_size

        def take_block(values):
            return lax.dynamic_slice_in_dim(values, block_start, block_size, 1)

        vis_now = take_block(visibilities)
        tiles_now = take_block(uv_tiles)
        offsets_now = take_block(kernel_offsets)
        row_start = tap_count * tiles_now[0] + offsets_now[0]
        col_start = tap_count * tiles_now[1] + offsets_now[1]
        kern_rows = lookup(offsets_now[0])
        kern_cols = lookup(offsets_now[1])
        row_delta = row_ids - row_start[:, None]
        col_delta = (col_ids - col_start[:, None]) % grid_side
        row_weight = jnp.zeros(row_ids.shape, jnp.float32)
        col_weight = jnp.zeros(col_ids.shape, jnp.float32)
        for tap_index in range(tap_count):
            row_weight = jnp.where(
                row_delta == tap_index, kern_rows[:, tap_index : tap_index + 1], row_weight
            )
            col_weight = jnp.where(
                col_delta == tap_index, kern_cols[:, tap_index : tap_index + 1], col_weight
            )
        row_weight = row_weight.astype(jnp.bfloat16)
        col_values = jnp.concatenate(
            [
                (vis_now[0][:, None] * col_weight).astype(jnp.bfloat16),
                (vis_now[1][:, None] * col_weight).astype(jnp.bfloat16),
            ],
            axis=1,
        )
        return accumulated + lax.dot_general(
            row_weight, col_values, (((0,), (0,)), ((), ())), preferred_element_type=jnp.float32
        )

    initial = jnp.zeros((window_rows, 2 * grid_side), jnp.float32)
    return lax.fori_loop(0, vis_count // block_size, add_block, initial)


def row_spectra(row_slab, rows_count, height, grid_side):
    line_count = row_slab.shape[0]
    real_part = row_slab[:, :grid_side].reshape(line_count, height, rows_count)
    imag_part = row_slab[:, grid_side:].reshape(line_count, height, rows_count)
    section_one = complex_einsum(
        "jrm,rk->jkm", (real_part, imag_part), phase_table(height, height, height)
    )
    turned = complex_scale(section_one, phase_table(height, rows_count, grid_side))
    return complex_einsum("jkm,mq->qkj", turned, phase_table(rows_count, rows_count, rows_count))


def column_spectra(columns, layout, rows_count, group_count, height, grid_side):
    columns_dev = height // group_count
    turned_layout = layout.replace("r", "k")
    section_one = complex_einsum(
        layout + ",rk->" + turned_layout, columns, phase_table(rows_count, rows_count, rows_count)
    )
    twiddles = tuple(
        (
            t.reshape(rows_count, group_count, columns_dev)
            for t in phase_table(rows_count, height, grid_side)
        )
    )
    twiddles = tuple((t[:, :, None] for t in twiddles))
    turned = complex_scale(section_one, twiddles)
    section_table = tuple(
        (t.reshape(group_count, columns_dev, height) for t in phase_table(height, height, height))
    )
    result = complex_einsum(turned_layout + ",gjq->cqk", turned, section_table)
    inverse_side = 1.0 / grid_side
    return jnp.stack(
        [part_out.reshape(columns_dev, grid_side) * inverse_side for part_out in result]
    )


def shards(visibilities, uv_tiles, kernel_offsets, kernel):
    rows_count = lax.axis_size("rows")
    group_count = lax.axis_size("grp")
    grid_side = G
    height = grid_side // rows_count
    columns_dev = height // group_count
    tap_count = kernel.shape[0]
    block_size = min(vis_block, visibilities.shape[1])
    row_base = lax.axis_index("rows") * height
    row_list = row_base + jnp.arange(height + tap_count, dtype=jnp.int32)
    partial_grid = grid_window(
        visibilities, uv_tiles, kernel_offsets, kernel, row_list, grid_side, block_size
    )
    main_rows = partial_grid[:height]
    tail_rows = partial_grid[height:]
    spill_rows = passed_along(tail_rows, "rows", 1)
    row_slab = jnp.concatenate([main_rows[:tap_count] + spill_rows, main_rows[tap_count:]], axis=0)
    own_rows = lax.psum_scatter(row_slab, "grp", scatter_dimension=0, tiled=True)
    spectra = row_spectra(own_rows, rows_count, height, grid_side)
    send_blocks = tuple(
        (p.reshape(rows_count, group_count, columns_dev * columns_dev) for p in spectra)
    )
    received = lax.all_to_all(
        lax.all_to_all(send_blocks, "rows", split_axis=0, concat_axis=0, tiled=True),
        "grp",
        split_axis=1,
        concat_axis=1,
        tiled=True,
    )
    columns = tuple(
        (p.reshape(rows_count, group_count, columns_dev, columns_dev) for p in received)
    )
    layout = "rgcj"
    return column_spectra(columns, layout, rows_count, group_count, height, grid_side)


def solution(mesh):
    in_specs = (P(None, ("rows", "grp")), P(None, ("rows", "grp")), P(None, ("rows", "grp")), P())
    out_specs = P(None, ("rows", "grp"), None)
    return jax.shard_map(shards, mesh=mesh, in_specs=in_specs, out_specs=out_specs, check_vma=False)
```

profile of v0, /device:TPU:0, one launch (start us, length us, event | category | flops | bytes accessed | tf_op | source)
XLA Modules:
  0.0 812.4 jit_solution(4082241112964909501)
XLA Ops:
  6.5 340.1 %while.17 = (s32[]{:T(128)}, f32[520,8192]{1,0:T(8,128)}, s32[2,4096]{1,0:T(2,128)}, s32[2,4096]{1,0:T(2,128)}, f32[8,8]{1,0:T(8,128)}, /*index=5*/f32[2,4096]{1...) while((s32[]{:T(128)}, f32[520,8192]{1,0:T(8,128)}, ...), condition=%wide.region_1.2_spmd.clone.clone, body=%wide.region_0.1_spmd.clone.clone.sunk | while | flops 2234162176 | bytes 42560240 | solution.py:92
  10.2 5.6 multiply_convert_fusion.3
  15.8 8.8 %select_add_fusion.2 = f32[520,8192]{1,0:T(8,128)} fusion(f32[520,8192]{1,0:T(8,128)} %get-tuple-element.437, pred[]{:T(512)S(6)} %compare.19, bf16[256,4096]{1,0:T(8,128)(2,1)S(1)} %get-tuple-element.412, bf16[256,4096]{1,0:T(8,128)(2,1)S(1)} %get-tuple-element.413, s32[520]{0:T(1024)S(1)} %get-tuple-element.454, f32[256]{0:T(256)S(1)} %bitcast.191, ...), kind=kOutput, calls=%fused_computation.3.clone.1 | convolution fusion | flops 2200209408 | bytes 38284320 | tf_op jit(solution)/shard_map/while/body/eval_jaxpr/dot_general | solution.py:87
  28.2 5.6 multiply_convert_fusion.3
  33.9 12.2 %select_add_fusion.2 = f32[520,8192]{1,0:T(8,128)} fusion(f32[520,8192]{1,0:T(8,128)} %get-tuple-element.437, pred[]{:T(512)S(6)} %compare.19, bf16[256,4096]{1,0:T(8,128)(2,1)S(1)} %get-tuple-element.412, bf16[256,4096]{1,0:T(8,128)(2,1)S(1)} %get-tuple-element.413, s32[520]{0:T(1024)S(1)} %get-tuple-element.454, f32[256]{0:T(256)S(1)} %bitcast.191, ...), kind=kOutput, calls=%fused_computation.3.clone.1 | convolution fusion | flops 2200209408 | bytes 38284320 | tf_op jit(solution)/shard_map/while/body/eval_jaxpr/dot_general | solution.py:87
  49.7 5.6 multiply_convert_fusion.3
  55.3 12.2 %select_add_fusion.2 = f32[520,8192]{1,0:T(8,128)} fusion(f32[520,8192]{1,0:T(8,128)} %get-tuple-element.437, pred[]{:T(512)S(6)} %compare.19, bf16[256,4096]{1,0:T(8,128)(2,1)S(1)} %get-tuple-element.412, bf16[256,4096]{1,0:T(8,128)(2,1)S(1)} %get-tuple-element.413, s32[520]{0:T(1024)S(1)} %get-tuple-element.454, f32[256]{0:T(256)S(1)} %bitcast.191, ...), kind=kOutput, calls=%fused_computation.3.clone.1 | convolution fusion | flops 2200209408 | bytes 38284320 | tf_op jit(solution)/shard_map/while/body/eval_jaxpr/dot_general | solution.py:87
  71.2 5.6 multiply_convert_fusion.3
  76.8 12.2 %select_add_fusion.2 = f32[520,8192]{1,0:T(8,128)} fusion(f32[520,8192]{1,0:T(8,128)} %get-tuple-element.437, pred[]{:T(512)S(6)} %compare.19, bf16[256,4096]{1,0:T(8,128)(2,1)S(1)} %get-tuple-element.412, bf16[256,4096]{1,0:T(8,128)(2,1)S(1)} %get-tuple-element.413, s32[520]{0:T(1024)S(1)} %get-tuple-element.454, f32[256]{0:T(256)S(1)} %bitcast.191, ...), kind=kOutput, calls=%fused_computation.3.clone.1 | convolution fusion | flops 2200209408 | bytes 38284320 | tf_op jit(solution)/shard_map/while/body/eval_jaxpr/dot_general | solution.py:87
  92.6 5.6 multiply_convert_fusion.3
  98.3 12.2 %select_add_fusion.2 = f32[520,8192]{1,0:T(8,128)} fusion(f32[520,8192]{1,0:T(8,128)} %get-tuple-element.437, pred[]{:T(512)S(6)} %compare.19, bf16[256,4096]{1,0:T(8,128)(2,1)S(1)} %get-tuple-element.412, bf16[256,4096]{1,0:T(8,128)(2,1)S(1)} %get-tuple-element.413, s32[520]{0:T(1024)S(1)} %get-tuple-element.454, f32[256]{0:T(256)S(1)} %bitcast.191, ...), kind=kOutput, calls=%fused_computation.3.clone.1 | convolution fusion | flops 2200209408 | bytes 38284320 | tf_op jit(solution)/shard_map/while/body/eval_jaxpr/dot_general | solution.py:87
  114.1 5.6 multiply_convert_fusion.3
  119.7 12.2 %select_add_fusion.2 = f32[520,8192]{1,0:T(8,128)} fusion(f32[520,8192]{1,0:T(8,128)} %get-tuple-element.437, pred[]{:T(512)S(6)} %compare.19, bf16[256,4096]{1,0:T(8,128)(2,1)S(1)} %get-tuple-element.412, bf16[256,4096]{1,0:T(8,128)(2,1)S(1)} %get-tuple-element.413, s32[520]{0:T(1024)S(1)} %get-tuple-element.454, f32[256]{0:T(256)S(1)} %bitcast.191, ...), kind=kOutput, calls=%fused_computation.3.clone.1 | convolution fusion | flops 2200209408 | bytes 38284320 | tf_op jit(solution)/shard_map/while/body/eval_jaxpr/dot_general | solution.py:87
  135.6 5.6 multiply_convert_fusion.3
  141.2 12.2 %select_add_fusion.2 = f32[520,8192]{1,0:T(8,128)} fusion(f32[520,8192]{1,0:T(8,128)} %get-tuple-element.437, pred[]{:T(512)S(6)} %compare.19, bf16[256,4096]{1,0:T(8,128)(2,1)S(1)} %get-tuple-element.412, bf16[256,4096]{1,0:T(8,128)(2,1)S(1)} %get-tuple-element.413, s32[520]{0:T(1024)S(1)} %get-tuple-element.454, f32[256]{0:T(256)S(1)} %bitcast.191, ...), kind=kOutput, calls=%fused_computation.3.clone.1 | convolution fusion | flops 2200209408 | bytes 38284320 | tf_op jit(solution)/shard_map/while/body/eval_jaxpr/dot_general | solution.py:87
  157.0 5.6 multiply_convert_fusion.3
  162.7 12.2 %select_add_fusion.2 = f32[520,8192]{1,0:T(8,128)} fusion(f32[520,8192]{1,0:T(8,128)} %get-tuple-element.437, pred[]{:T(512)S(6)} %compare.19, bf16[256,4096]{1,0:T(8,128)(2,1)S(1)} %get-tuple-element.412, bf16[256,4096]{1,0:T(8,128)(2,1)S(1)} %get-tuple-element.413, s32[520]{0:T(1024)S(1)} %get-tuple-element.454, f32[256]{0:T(256)S(1)} %bitcast.191, ...), kind=kOutput, calls=%fused_computation.3.clone.1 | convolution fusion | flops 2200209408 | bytes 38284320 | tf_op jit(solution)/shard_map/while/body/eval_jaxpr/dot_general | solution.py:87
  178.5 5.6 multiply_convert_fusion.3
  184.1 12.2 %select_add_fusion.2 = f32[520,8192]{1,0:T(8,128)} fusion(f32[520,8192]{1,0:T(8,128)} %get-tuple-element.437, pred[]{:T(512)S(6)} %compare.19, bf16[256,4096]{1,0:T(8,128)(2,1)S(1)} %get-tuple-element.412, bf16[256,4096]{1,0:T(8,128)(2,1)S(1)} %get-tuple-element.413, s32[520]{0:T(1024)S(1)} %get-tuple-element.454, f32[256]{0:T(256)S(1)} %bitcast.191, ...), kind=kOutput, calls=%fused_computation.3.clone.1 | convolution fusion | flops 2200209408 | bytes 38284320 | tf_op jit(solution)/shard_map/while/body/eval_jaxpr/dot_general | solution.py:87
  200.0 5.6 multiply_convert_fusion.3
  205.6 12.2 %select_add_fusion.2 = f32[520,8192]{1,0:T(8,128)} fusion(f32[520,8192]{1,0:T(8,128)} %get-tuple-element.437, pred[]{:T(512)S(6)} %compare.19, bf16[256,4096]{1,0:T(8,128)(2,1)S(1)} %get-tuple-element.412, bf16[256,4096]{1,0:T(8,128)(2,1)S(1)} %get-tuple-element.413, s32[520]{0:T(1024)S(1)} %get-tuple-element.454, f32[256]{0:T(256)S(1)} %bitcast.191, ...), kind=kOutput, calls=%fused_computation.3.clone.1 | convolution fusion | flops 2200209408 | bytes 38284320 | tf_op jit(solution)/shard_map/while/body/eval_jaxpr/dot_general | solution.py:87
  221.4 5.6 multiply_convert_fusion.3
  227.0 12.2 %select_add_fusion.2 = f32[520,8192]{1,0:T(8,128)} fusion(f32[520,8192]{1,0:T(8,128)} %get-tuple-element.437, pred[]{:T(512)S(6)} %compare.19, bf16[256,4096]{1,0:T(8,128)(2,1)S(1)} %get-tuple-element.412, bf16[256,4096]{1,0:T(8,128)(2,1)S(1)} %get-tuple-element.413, s32[520]{0:T(1024)S(1)} %get-tuple-element.454, f32[256]{0:T(256)S(1)} %bitcast.191, ...), kind=kOutput, calls=%fused_computation.3.clone.1 | convolution fusion | flops 2200209408 | bytes 38284320 | tf_op jit(solution)/shard_map/while/body/eval_jaxpr/dot_general | solution.py:87
  242.9 5.6 multiply_convert_fusion.3
  248.5 12.2 %select_add_fusion.2 = f32[520,8192]{1,0:T(8,128)} fusion(f32[520,8192]{1,0:T(8,128)} %get-tuple-element.437, pred[]{:T(512)S(6)} %compare.19, bf16[256,4096]{1,0:T(8,128)(2,1)S(1)} %get-tuple-element.412, bf16[256,4096]{1,0:T(8,128)(2,1)S(1)} %get-tuple-element.413, s32[520]{0:T(1024)S(1)} %get-tuple-element.454, f32[256]{0:T(256)S(1)} %bitcast.191, ...), kind=kOutput, calls=%fused_computation.3.clone.1 | convolution fusion | flops 2200209408 | bytes 38284320 | tf_op jit(solution)/shard_map/while/body/eval_jaxpr/dot_general | solution.py:87
  264.4 5.6 multiply_convert_fusion.3
  270.0 12.2 %select_add_fusion.2 = f32[520,8192]{1,0:T(8,128)} fusion(f32[520,8192]{1,0:T(8,128)} %get-tuple-element.437, pred[]{:T(512)S(6)} %compare.19, bf16[256,4096]{1,0:T(8,128)(2,1)S(1)} %get-tuple-element.412, bf16[256,4096]{1,0:T(8,128)(2,1)S(1)} %get-tuple-element.413, s32[520]{0:T(1024)S(1)} %get-tuple-element.454, f32[256]{0:T(256)S(1)} %bitcast.191, ...), kind=kOutput, calls=%fused_computation.3.clone.1 | convolution fusion | flops 2200209408 | bytes 38284320 | tf_op jit(solution)/shard_map/while/body/eval_jaxpr/dot_general | solution.py:87
  285.8 5.6 multiply_convert_fusion.3
  291.4 12.2 %select_add_fusion.2 = f32[520,8192]{1,0:T(8,128)} fusion(f32[520,8192]{1,0:T(8,128)} %get-tuple-element.437, pred[]{:T(512)S(6)} %compare.19, bf16[256,4096]{1,0:T(8,128)(2,1)S(1)} %get-tuple-element.412, bf16[256,4096]{1,0:T(8,128)(2,1)S(1)} %get-tuple-element.413, s32[520]{0:T(1024)S(1)} %get-tuple-element.454, f32[256]{0:T(256)S(1)} %bitcast.191, ...), kind=kOutput, calls=%fused_computation.3.clone.1 | convolution fusion | flops 2200209408 | bytes 38284320 | tf_op jit(solution)/shard_map/while/body/eval_jaxpr/dot_general | solution.py:87
  307.3 5.6 multiply_convert_fusion.3
  312.9 12.2 %select_add_fusion.2 = f32[520,8192]{1,0:T(8,128)} fusion(f32[520,8192]{1,0:T(8,128)} %get-tuple-element.437, pred[]{:T(512)S(6)} %compare.19, bf16[256,4096]{1,0:T(8,128)(2,1)S(1)} %get-tuple-element.412, bf16[256,4096]{1,0:T(8,128)(2,1)S(1)} %get-tuple-element.413, s32[520]{0:T(1024)S(1)} %get-tuple-element.454, f32[256]{0:T(256)S(1)} %bitcast.191, ...), kind=kOutput, calls=%fused_computation.3.clone.1 | convolution fusion | flops 2200209408 | bytes 38284320 | tf_op jit(solution)/shard_map/while/body/eval_jaxpr/dot_general | solution.py:87
  328.7 5.6 multiply_convert_fusion.3
  334.4 12.2 %select_add_fusion.2 = f32[520,8192]{1,0:T(8,128)} fusion(f32[520,8192]{1,0:T(8,128)} %get-tuple-element.437, pred[]{:T(512)S(6)} %compare.19, bf16[256,4096]{1,0:T(8,128)(2,1)S(1)} %get-tuple-element.412, bf16[256,4096]{1,0:T(8,128)(2,1)S(1)} %get-tuple-element.413, s32[520]{0:T(1024)S(1)} %get-tuple-element.454, f32[256]{0:T(256)S(1)} %bitcast.191, ...), kind=kOutput, calls=%fused_computation.3.clone.1 | convolution fusion | flops 2200209408 | bytes 38284320 | tf_op jit(solution)/shard_map/while/body/eval_jaxpr/dot_general | solution.py:87
  350.6 19.6 %copy.39 = f32[520,8192]{0,1:T(8,128)} copy(f32[520,8192]{1,0:T(8,128)} %get-tuple-element.229) | data formatting | bytes 34078720 | tf_op jit(solution)/shard_map/while | solution.py:92
  370.2 13.7 %slice.305 = f32[504,8192]{0,1:T(8,128)} slice(f32[520,8192]{0,1:T(8,128)} %copy.39), slice={[8:512], [0:8192]} | slice | bytes 33030144 | tf_op jit(solution)/shard_map/slice | solution.py:146
  387.5 13.5 %pad_maximum_fusion = f32[512,8192]{0,1:T(8,128)} fusion(f32[504,8192]{0,1:T(8,128)} %slice.305, f32[8,8192]{0,1:T(8,128)} %copy.40), kind=kLoop, calls=%fused_computation.66 | loop fusion | flops 4194304 | bytes 33554432 | tf_op jit(solution)/shard_map/concatenate | solution.py:146
  401.2 125.2 %reduce-scatter.2.cloned.1.call-done = f32[128,8192]{0,1:T(8,128)} async-done(((f32[512,8192]{0,1:T(8,128)}), f32[128,8192]{0,1:T(8,128)}) %reduce-scatter.2.cloned.1.call-update) | async-done | bytes 4194320 | tf_op jit(solution)/shard_map/reduce_scatter | solution.py:147
  526.4 3.8 slice_bitcast_fusion
  532.3 10.4 %fusion.84 = f32[512,128,8]{1,0,2:T(8,128)} fusion(f32[128,512,8]{1,0,2:T(8,128)} %copy.41), kind=kOutput, calls=%fused_computation.118 | convolution fusion | flops 3224895488 | bytes 4194304 | tf_op jit(solution)/shard_map/jrm,rk->jkm/dot_general | solution.py:29
  542.7 9.1 %fusion.88 = f32[512,128,8]{1,0,2:T(8,128)} fusion(f32[128,512,8]{1,0,2:T(8,128)S(1)} %copy-done.5), kind=kOutput, calls=%fused_computation.122 | convolution fusion | flops 3224895488 | bytes 4194304 | tf_op jit(solution)/shard_map/jrm,rk->jkm/dot_general | solution.py:29
  553.7 9.1 %convolution_add_fusion = f32[512,128,8]{1,0,2:T(8,128)S(1)} fusion(f32[512,128,8]{1,0,2:T(8,128)} %fusion.84, f32[128,512,8]{1,0,2:T(8,128)S(1)} %copy.42), kind=kOutput, calls=%fused_computation.102 | convolution fusion | flops 3225419776 | bytes 6291456 | tf_op jit(solution)/shard_map/jrm,rk->jkm/dot_general | solution.py:29
  562.8 10.2 %add_bitcast_fusion.1 = (f32[128,512,8]{0,1,2:T(8,128)}, f32[128,512,8]{0,1,2:T(8,128)}) fusion(f32[512,128,8]{1,0,2:T(8,128)S(1)} %convolution_add_fusion, f32[512,8]{0,1:T(8,128)S(1)} %get-tuple-element.331, f32[512,8]{0,1:T(8,128)S(1)} %get-tuple-element.332, f32[512,128,8]{1,0,2:T(8,128)S(1)} %copy-done.4, f32[128,512,8]{1,0,2:T(8,128)S(1)} %copy.42), kind=kOutput, calls=%fused_computation.90 | convolution fusion | flops 3228565504 | bytes 10518528 | tf_op jit(solution)/shard_map/jrm,rk->jkm/dot_general | solution.py:29
  578.3 3.4 fusion.133
  581.7 3.3 add_bitcast_fusion
  591.1 5.8 all-to-all-start.2
  596.9 3.4 fusion.137
  600.3 3.3 subtract_bitcast_fusion
  607.5 37.5 %all-to-all-done.2 = f32[8,4,16384]{2,1,0:T(4,128)} async-done(((f32[8,4,16384]{2,1,0:T(4,128)}), f32[8,4,16384]{2,1,0:T(4,128)}, u32[]{:S(2)}, u32[]{:S(2)}) %all-to-all-start.2) | async-done | bytes 2097184 | tf_op jit(solution)/shard_map/all_to_all | solution.py:153
  645.0 3.6 all-to-all-start
  648.6 4.1 copy.53
  652.8 44.3 %all-to-all-done = f32[8,4,16384]{2,1,0:T(4,128)S(1)} async-done(((f32[8,4,16384]{2,1,0:T(4,128)}), f32[8,4,16384]{2,1,0:T(4,128)S(1)}, u32[]{:S(2)}, u32[]{:S(2)}) %all-to-all-start) | async-done | bytes 2097184 | tf_op jit(solution)/shard_map/all_to_all | solution.py:153
  698.4 3.6 all-to-all-start.3
  702.0 4.1 copy.48
  706.1 21.5 %all-to-all-done.3 = f32[8,4,16384]{2,0,1:T(8,128)S(1)} async-done(((f32[8,4,16384]{2,0,1:T(8,128)}), f32[8,4,16384]{2,0,1:T(8,128)S(1)}, u32[]{:S(2)}, u32[]{:S(2)}) %all-to-all-start.3) | async-done | bytes 2097184 | tf_op jit(solution)/shard_map/all_to_all | solution.py:152
  728.9 4.0 all-to-all-start.1
  733.1 4.9 fusion.50
  737.9 3.2 fusion.52
  741.1 17.1 %all-to-all-done.1 = f32[8,4,16384]{2,0,1:T(8,128)S(1)} async-done(((f32[8,4,16384]{2,0,1:T(8,128)}), f32[8,4,16384]{2,0,1:T(8,128)S(1)}, u32[]{:S(2)}, u32[]{:S(2)}) %all-to-all-start.1) | async-done | bytes 2097184 | tf_op jit(solution)/shard_map/all_to_all | solution.py:152
  758.2 3.7 fusion.66
  764.3 7.6 fusion.58
  771.8 7.4 fusion.60
  779.3 7.7 fusion.49
  787.0 7.8 fusion.47
  799.5 5.6 copy.63
  (164 shorter events, 94.3 us)
Async XLA Ops:
  6.5 519.9 %reduce-scatter.2.cloned.1.call-start = ((), (), s32[]{:S(2)}) async-start(), calls=%async_computation.5 | async-start | bytes 20971520 | tf_op jit(solution)/shard_map/reduce_scatter | solution.py:147
  347.6 36.3 %collective-permute-start = (f32[8,8192]{1,0:T(8,128)S(1)}, f32[8,8192]{1,0:T(8,128)S(1)}, u32[]{:S(2)}, u32[]{:S(2)}) collective-permute-start(f32[8,8192]{1,0:T(8,128)S(1)} %slice.241), channel_id=1, source_target_pairs={{0,4},{4,8},{8,12},{12,16},{16,20},{20,24},{24,28},{28,0},{1,5},{5... | collective-permute-start | bytes 786440 | tf_op jit(solution)/shard_map/ppermute | solution.py:16
  532.3 10.4 %copy-start.5 = (f32[128,512,8]{1,0,2:T(8,128)S(1)}, f32[128,512,8]{1,0,2:T(8,128)}, u32[]{:S(2)}) copy-start(f32[128,512,8]{1,0,2:T(8,128)} %copy.41) | copy-start | bytes 6291460
  553.7 9.1 %copy-start.4 = (f32[512,128,8]{1,0,2:T(8,128)S(1)}, f32[512,128,8]{1,0,2:T(8,128)}, u32[]{:S(2)}) copy-start(f32[512,128,8]{1,0,2:T(8,128)} %fusion.88) | copy-start | bytes 6291460
  591.1 53.9 %all-to-all-start.2 = ((f32[8,4,16384]{2,1,0:T(4,128)}), f32[8,4,16384]{2,1,0:T(4,128)}, u32[]{:S(2)}, u32[]{:S(2)}) async-start(f32[8,4,16384]{2,1,0:T(4,128)} %reshape.179), calls=%async_computation.3 | async-start | bytes 4194304 | tf_op jit(solution)/shard_map/all_to_all | solution.py:153
  645.0 52.1 %all-to-all-start = ((f32[8,4,16384]{2,1,0:T(4,128)}), f32[8,4,16384]{2,1,0:T(4,128)S(1)}, u32[]{:S(2)}, u32[]{:S(2)}) async-start(f32[8,4,16384]{2,1,0:T(4,128)} %reshape.177), calls=%async_computation.1 | async-start | bytes 4194304 | tf_op jit(solution)/shard_map/all_to_all | solution.py:153
  697.1 1.3 copy-start.3
  698.4 29.2 %all-to-all-start.3 = ((f32[8,4,16384]{2,0,1:T(8,128)}), f32[8,4,16384]{2,0,1:T(8,128)S(1)}, u32[]{:S(2)}, u32[]{:S(2)}) async-start(f32[8,4,16384]{2,0,1:T(8,128)} %copy.53), calls=%async_computation.4 | async-start | bytes 4194304 | tf_op jit(solution)/shard_map/all_to_all | solution.py:152
  727.6 1.3 copy-start
  728.9 29.2 %all-to-all-start.1 = ((f32[8,4,16384]{2,0,1:T(8,128)}), f32[8,4,16384]{2,0,1:T(8,128)S(1)}, u32[]{:S(2)}, u32[]{:S(2)}) async-start(f32[8,4,16384]{2,0,1:T(8,128)} %copy.48), calls=%async_computation.2 | async-start | bytes 4194304 | tf_op jit(solution)/shard_map/all_to_all | solution.py:152
  733.0 4.9 copy-start.1
  758.2 3.7 copy-start.2
Sparse Core Ops, SparseCore 0:
  401.2 125.1 reduce-scatter.1
where the time goes:
time: 822 us; the launch traced here: 812 us
  matrix products  318 us (39%)
  waiting for transfers between devices  246 us (30%)
  other arithmetic  120 us (15%)
  local copies, waits for them, and re-layouts  94.3 us (11%)
  starting transfers between devices  20.1 us (2%)
  between operations  14 us (2%)
    dot_general x16, matrix products, add_block(): lax.dot_general(row_weight, col_values, (((0,), (0,)), ((), ())), preferr...  192 us
    reduce_scatter x1, waiting for transfers between devices, shards(): lax.psum_scatter(row_slab, 'grp', scatter_dimension=0, tiled=True)  125 us
    dot_general x16, matrix products, product(): jnp.einsum(pattern, left_one, right_one, precision=lax.Precision.HIGHEST)  96.9 us
    convert_element_type x16, other arithmetic, add_block(): (vis_now[0][:, None] * col_weight).astype(jnp.bfloat16)  89.9 us
    all_to_all x2, waiting for transfers between devices, shards(): lax.all_to_all(send_blocks, 'rows', split_axis=0, concat_axis=0, tiled=True)  81.8 us
    all_to_all x2, waiting for transfers between devices, shards(): lax.all_to_all(lax.all_to_all(send_blocks, 'rows', split_axis=0, concat_a...  38.6 us
    dot_general x32, matrix products, lookup(): return jnp.dot(one_hot, kernel, precision=lax.Precision.HIGHEST)  28.6 us
    while x1, local copies, waits for them, and re-layouts, grid_window(): return lax.fori_loop(0, vis_count // block_size, add_block, initial)  19.6 us
  transfers between devices with their start and end apart: 6, of which 5 were waited for; matrix products, arithmetic and copies ran while one was open for 7% of the time, Pallas kernels for 0%

commit v1 on v0

v1 whole, which is shorter than its diff:
```python
import functools
import math

import jax
import jax.numpy as jnp
from jax import lax
from jax.experimental import pallas as pl
from jax.experimental.pallas import tpu as pltpu
from jax.sharding import PartitionSpec as P

G = 4096
SEGMENT = 64
WINDOW = 16
vis_block = 1024


def phases(first, second, length):
    angles = (first * second % length).astype(jnp.float32) * (2.0 * math.pi / length)
    return jnp.cos(angles), jnp.sin(angles)


def periodic(window, tile):
    half = WINDOW // 2
    swapped = jnp.concatenate([window[half:], window[:half]], axis=0)
    pattern = jnp.where((tile & 1) == 1, swapped, window)
    upper = lax.broadcasted_iota(jnp.int32, window.shape, 0) // half
    block = (tile - upper + 1) >> 1
    return pattern.astype(jnp.bfloat16), block.astype(jnp.float32).astype(jnp.bfloat16)


def grid_kernel(group_count, steps_per_block, slab, lines, period, segments, data_ref, taps_ref, table_ref, out_ref, total):
    step = pl.program_id(0)
    side = total.shape[0] - WINDOW
    seg_blocks = SEGMENT // WINDOW + 1

    @pl.when(step == 0)
    def _():
        total[...] = jnp.zeros_like(total)

    slab_index = step // (steps_per_block * group_count)
    base = slab_index * slab
    vis_re = data_ref[0, 0:1, :]
    vis_im = data_ref[0, 1:2, :]
    row_start = data_ref[0, 2:3, :].astype(jnp.int32) - base
    col_start = data_ref[0, 3:4, :].astype(jnp.int32)
    count = vis_re.shape[1]
    shape = (WINDOW, count)
    row_offset, row_tile = row_start & 7, row_start >> 3
    col_offset, col_tile = col_start & 7, col_start >> 3
    row_window = jnp.zeros(shape, jnp.float32)
    col_window = jnp.zeros(shape, jnp.float32)
    for offset in range(taps_ref.shape[0]):
        taps = jnp.broadcast_to(taps_ref[offset], shape)
        row_window = jnp.where(row_offset == offset, taps, row_window)
        col_window = jnp.where(col_offset == offset, taps, col_window)
    zero = jnp.zeros(shape, jnp.bfloat16)

    per_segment = SEGMENT // 8
    col_low, col_seg = col_tile & (per_segment - 1), col_tile // per_segment
    pattern_re, col_block = periodic(vis_re * col_window, col_low)
    pattern_im, _ = periodic(vis_im * col_window, col_low)
    seg_delta = jnp.broadcast_to(col_seg, shape) - lax.broadcasted_iota(jnp.int32, shape, 0)
    seg_delta = seg_delta.astype(jnp.float32).astype(jnp.bfloat16)
    one = jnp.ones(shape, jnp.bfloat16)
    weights_re = [jnp.where(col_block == i, pattern_re, zero) for i in range(seg_blocks)]
    weights_im = [jnp.where(col_block == i, pattern_im, zero) for i in range(seg_blocks)]
    hot = [jnp.where(seg_delta == i * WINDOW, one, zero) for i in range(segments // WINDOW)]
    weights = jnp.concatenate(weights_re + weights_im + hot, axis=0)
    parts = seg_blocks * WINDOW
    inner = jnp.dot(
        table_ref[: 2 * lines, : 2 * parts], weights[: 2 * parts], preferred_element_type=jnp.float32
    )
    outer = jnp.dot(
        table_ref[2 * lines :, 2 * parts :], weights[2 * parts :], preferred_element_type=jnp.float32
    )
    turn_re, turn_im = outer[:period], outer[period:]
    reals, imags = [], []
    for first in range(0, lines, period):
        in_re = inner[first : first + period]
        in_im = inner[lines + first : lines + first + period]
        reals.append((in_re * turn_re - in_im * turn_im).astype(jnp.bfloat16))
        imags.append((in_re * turn_im + in_im * turn_re).astype(jnp.bfloat16))
    spectra = jnp.concatenate(reals + imags, axis=0)

    row_pattern, row_block = periodic(row_window, row_tile)
    row_weights = jnp.concatenate(
        [jnp.where(row_block == i, row_pattern, zero) for i in range(slab // WINDOW + 1)], axis=0
    )
    rows = pl.ds(pl.multiple_of(base, WINDOW), slab + WINDOW)
    total[rows, :] += lax.dot_general(
        row_weights, spectra, (((1,), (1,)), ((), ())), preferred_element_type=jnp.float32
    )

    @pl.when(step == pl.num_programs(0) - 1)
    def _():
        total[:WINDOW, :] += total[side:, :]
        out_ref[0] = total[:side, :lines]
        out_ref[1] = total[:side, lines:]


def line_spectra(gathered, kernel, first_line, lines, group_count, slab, side):
    device_count, _, vis_count = gathered.shape
    block = min(vis_block, vis_count)
    steps = vis_count // block
    segments = side // SEGMENT
    period = min(segments, lines)
    tap_count = kernel.shape[0]
    offsets = jnp.arange(tap_count)[:, None]
    places = jnp.arange(WINDOW)[None, :] - offsets
    inside = (places >= 0) & (places < tap_count)
    taps = jnp.where(inside, kernel[offsets, jnp.clip(places, 0, tap_count - 1)], 0.0)[:, :, None]

    line_ids = first_line + jnp.arange(lines, dtype=jnp.int32)[:, None]
    in_cos, in_sin = phases(line_ids, jnp.arange(SEGMENT + WINDOW, dtype=jnp.int32)[None, :], side)
    out_cos, out_sin = phases(line_ids[:period], jnp.arange(segments, dtype=jnp.int32)[None, :], segments)
    inner = jnp.block([[in_cos, -in_sin], [in_sin, in_cos]])
    outer = jnp.concatenate([out_cos, out_sin], axis=0)
    table = jnp.concatenate(
        [
            jnp.pad(inner, ((0, 0), (0, segments))),
            jnp.pad(outer, ((0, 0), (inner.shape[1], 0))),
        ],
        axis=0,
    ).astype(jnp.bfloat16)
    body = functools.partial(grid_kernel, group_count, steps, slab, lines, period, segments)
    return pl.pallas_call(
        body,
        grid=(device_count * steps,),
        in_specs=[
            pl.BlockSpec((1, 4, block), lambda i: (i // steps, 0, i % steps)),
            pl.BlockSpec(taps.shape, lambda i: (0, 0, 0)),
            pl.BlockSpec(table.shape, lambda i: (0, 0)),
        ],
        out_specs=pl.BlockSpec((2, side, lines), lambda i: (0, 0, 0)),
        out_shape=jax.ShapeDtypeStruct((2, side, lines), jnp.float32),
        scratch_shapes=[pltpu.VMEM((side + WINDOW, 2 * lines), jnp.float32)],
        compiler_params=pltpu.CompilerParams(vmem_limit_bytes=60 * 2**20),
        name="line_spectra",
    )(gathered, taps, table)


def row_transform(spectra, lines, side):
    high = 128
    low = side // high
    grouped = spectra.reshape(2, high, low, lines)
    ids = jnp.arange(high, dtype=jnp.int32)
    cos, sin = phases(ids[:, None], ids[None, :], high)
    first = jnp.stack([jnp.stack([cos, sin]), jnp.stack([-sin, cos])])
    turned = jnp.einsum("cubl,ceuk->eblk", grouped, first, precision=lax.Precision.HIGH)
    low_ids = jnp.arange(low, dtype=jnp.int32)
    tw_cos, tw_sin = phases(low_ids[:, None], ids[None, :], side)
    tw_cos, tw_sin = tw_cos[:, None, :], tw_sin[:, None, :]
    turned = jnp.stack(
        [turned[0] * tw_cos - turned[1] * tw_sin, turned[0] * tw_sin + turned[1] * tw_cos]
    )
    cos, sin = phases(low_ids[:, None], low_ids[None, :], low)
    second = jnp.stack([jnp.stack([cos, sin]), jnp.stack([-sin, cos])]) * (1.0 / side)
    image = jnp.einsum(
        "eblk,ecbq->clqk", turned, second, precision=lax.Precision.HIGH
    )
    return image.reshape(2, lines, side)


def shards(visibilities, uv_tiles, kernel_offsets, kernel):
    rows_count = lax.axis_size("rows")
    group_count = lax.axis_size("grp")
    tap_count = kernel.shape[0]
    side = G
    slab = side // rows_count
    lines = slab // group_count
    starts = (tap_count * uv_tiles + kernel_offsets).astype(jnp.float32)
    packed = jnp.concatenate([visibilities, starts], axis=0)
    gathered = lax.all_gather(packed, ("rows", "grp"), axis=0, tiled=False)
    first_line = (lax.axis_index("rows") * group_count + lax.axis_index("grp")) * lines
    spectra = line_spectra(gathered, kernel, first_line, lines, group_count, slab, side)
    return row_transform(spectra, lines, side)


def solution(mesh):
    in_specs = (P(None, ("rows", "grp")), P(None, ("rows", "grp")), P(None, ("rows", "grp")), P())
    out_specs = P(None, ("rows", "grp"), None)
    return jax.shard_map(shards, mesh=mesh, in_specs=in_specs, out_specs=out_specs, check_vma=False)
```

time: 822 us -> 244 us (0.30); the launches traced: 812 us -> 244 us
  matrix products: 318 us -> 11.7 us
  waiting for transfers between devices: 246 us -> 55.9 us
  Pallas kernels: 0 us -> 142 us
  other arithmetic: 120 us -> 9.06 us
  local copies, waits for them, and re-layouts: 94.3 us -> 11.7 us
  starting transfers between devices: 20.1 us -> 0.01 us
    dot_general x64 -> x2, matrix products: 318 us -> 11.7 us  [the longest x1 6.09 us: row_transform(): jnp.einsum('eblk,ecbq->clqk', turned, second, precision=lax.Precision.HIGH)]
    pallas_call x0 -> x1, Pallas kernels: none -> 142 us  [line_spectra(): pl.pallas_call(body, grid=(device_count * steps,), in_specs=[pl.BlockSpec...]
    reduce_scatter x1 -> x0, waiting for transfers between devices: 125 us -> none  [shards(): lax.psum_scatter(row_slab, 'grp', scatter_dimension=0, tiled=True)]
    all_to_all x4 -> x0, waiting for transfers between devices: 120 us -> none  [the longest x2 81.8 us: shards(): lax.all_to_all(send_blocks, 'rows', split_axis=0, concat_axis=0, tiled=True)]
    convert_element_type x16 -> x1, other arithmetic: 89.9 us -> 0.81 us  [shards(): starts = (tap_count * uv_tiles + kernel_offsets).astype(jnp.float32)]
    all_gather x0 -> x1, waiting for transfers between devices: none -> 55.8 us  [shards(): gathered = lax.all_gather(packed, ('rows', 'grp'), axis=0, tiled=False)]
    slice x50 -> x0, local copies, waits for them, and re-layouts: 30.1 us -> none  [the longest x1 13.7 us: shards(): main_rows[tap_count:]]
    while x1 -> x0, local copies, waits for them, and re-layouts: 19.6 us -> none  [grid_window(): return lax.fori_loop(0, vis_count // block_size, add_block, initial)]
  transfers between devices with their start and end apart: 6 -> 1, of which waited for: 5 -> 1; matrix products, arithmetic and copies ran while one was open for 7% -> 2% of each run, Pallas kernels for 0% -> 0%
where the time goes in v1:
time: 244 us
  Pallas kernels  142 us (58%)
  waiting for transfers between devices  55.9 us (23%)
  between operations  13.5 us (6%)
  local copies, waits for them, and re-layouts  11.7 us (5%)
  matrix products  11.7 us (5%)
  other arithmetic  9.06 us (4%)
    pallas_call x1, Pallas kernels, line_spectra(): pl.pallas_call(body, grid=(device_count * steps,), in_specs=[pl.BlockSpec...  142 us
    all_gather x1, waiting for transfers between devices, shards(): gathered = lax.all_gather(packed, ('rows', 'grp'), axis=0, tiled=False)  55.8 us
    dot_general x1, matrix products, row_transform(): jnp.einsum('eblk,ecbq->clqk', turned, second, precision=lax.Precision.HIGH)  6.09 us
    dot_general x1, matrix products, row_transform(): jnp.einsum('cubl,ceuk->eblk', grouped, first, precision=lax.Precision.HIGH)  5.58 us
    another operation x1, local copies, waits for them, and re-layouts, row_transform(): jnp.stack([turned[0] * tw_cos - turned[1] * tw_sin, turned[0] * tw_sin +...  5.51 us
    reshape x1, local copies, waits for them, and re-layouts, row_transform(): return image.reshape(2, lines, side)  4.94 us
  transfers between devices with their start and end apart: 1, of which 1 were waited for; matrix products, arithmetic and copies ran while one was open for 2% of the time, Pallas kernels for 0%

profile of v1, /device:TPU:0, one launch (start us, length us, event | category | flops | bytes accessed | tf_op | source)
XLA Modules:
  0.0 243.7 jit_solution(8655344056872065324)
XLA Ops:
  6.5 0.0 copy-start
  6.5 0.0 all-gather.4.cloned.1.call-start
  6.5 0.8 add_convert_fusion
  7.4 1.4 maximum_bitcast_fusion.4
  8.8 0.0 all-gather.4.cloned.1.call-update
  8.8 0.2 fusion.32
  9.0 0.1 reshape.260
  9.1 0.0 copy-done
  9.1 1.0 gather_fusion
  10.1 0.2 gather.8
  10.4 0.1 fusion.75
  10.5 0.1 fusion.71
  10.5 0.1 fusion.73
  10.6 0.3 fusion.58
  10.9 0.2 cosine_convert_fusion.1
  11.1 0.1 fusion.28
  11.2 0.3 fusion.54
  11.5 0.3 negate_convert_fusion
  11.9 0.1 fusion.18
  12.0 0.7 pad_maximum_fusion.1.table_ref
  12.7 0.6 fusion.46.taps_ref
  13.3 55.8 %all-gather.4.cloned.1.call-done.data_ref = f32[32,4,4096]{2,1,0:T(4,128)} async-done(((f32[1,4,4096]{2,1,0:T(4,128)}), f32[32,4,4096]{2,1,0:T(4,128)}) %all-gather.4.cloned.1.call-update) | async-done | bytes 2097168 | tf_op jit(solution)/shard_map/all_gather | solution.py:173
  69.2 141.9 %line_spectra.1 = f32[2,4096,128]{2,1,0:T(8,128)} custom-call(f32[32,4,4096]{2,1,0:T(4,128)} %all-gather.4.cloned.1.call-done.data_ref, f32[8,16,1]{2,1,0:T(8,128)} %fusion.46.taps_ref, bf16[384,224]{1,0:T(8,128)(2,1)} %pad_maximum_fusion.1.table_ref), custom_call_target="tpu_custom_call" | custom-call | tf_op jit(solution)/shard_map/line_spectra/pallas_call | solution.py:126
  211.1 5.6 %fusion.5 = f32[2,32,128,128]{2,3,1,0:T(8,128)S(1)} fusion(f32[2,128,32,128]{3,2,1,0:T(8,128)} %bitcast.49, f32[1,2,128,128]{2,3,0,1:T(8,128)S(1)} %get-tuple-element.8, f32[1,2,128,128]{2,3,0,1:T(8,128)S(1)} %get-tuple-element.7), kind=kOutput, calls=%fused_computation.7 | convolution fusion | flops 1610678272 | bytes 8650752 | tf_op jit(solution)/shard_map/cubl,ceuk->eblk/dot_general | solution.py:149
  216.7 1.4 multiply_subtract_fusion
  218.1 2.3 pad_maximum_fusion
  220.4 5.5 %copy.24 = f32[2,32,128,128]{3,1,0,2:T(8,128)} copy(f32[2,32,128,128]{2,3,1,0:T(8,128)} %pad_maximum_fusion) | data formatting | bytes 8388608 | tf_op jit(solution)/shard_map/stack | solution.py:153
  225.9 6.1 %fusion.8 = f32[2,128,32,128]{3,2,1,0:T(8,128)} fusion(f32[2,32,128,128]{3,1,0,2:T(8,128)} %copy.24, f32[1,2,32,32]{2,3,0,1:T(8,128)S(1)} %get-tuple-element.10, f32[1,2,32,32]{2,3,0,1:T(8,128)S(1)} %get-tuple-element.9), kind=kOutput, calls=%fused_computation.8 | convolution fusion | flops 402661376 | bytes 8404992 | tf_op jit(solution)/shard_map/eblk,ecbq->clqk/dot_general | solution.py:158
  231.9 4.9 %reshape.259 = f32[2,128,4096]{2,1,0:T(8,128)} reshape(f32[2,128,32,128]{3,2,1,0:T(8,128)} %fusion.8) | data formatting | bytes 8388608 | tf_op jit(solution)/shard_map/reshape | solution.py:161
  (5 shorter events, 0.0 us)
Async XLA Ops:
  6.5 2.6 %copy-start = (f32[8,8]{1,0:T(8,128)S(1)}, f32[8,8]{1,0:T(8,128)}, u32[]{:S(2)}) copy-start(f32[8,8]{1,0:T(8,128)} %param.7) | copy-start | bytes 772
  6.5 62.7 %all-gather.4.cloned.1.call-start = ((), (), s32[]{:S(2)}) async-start(), calls=%async_computation | async-start | bytes 2162688 | tf_op jit(solution)/shard_map/all_gather | solution.py:173
Sparse Core Ops, SparseCore 0:
  10.2 58.9 all-gather.3

commit v2 on v1

--- a/solution.py
+++ b/solution.py
@@ -11,7 +11,7 @@
 G = 4096
 SEGMENT = 64
 WINDOW = 16
-vis_block = 1024
+vis_block = 2048
 
 
 def phases(first, second, length):

time: 244 us -> 219 us (0.90)
  Pallas kernels: 142 us -> 117 us
    pallas_call x1, Pallas kernels: 142 us -> 117 us  [line_spectra(): pl.pallas_call(body, grid=(device_count * steps,), in_specs=[pl.BlockSpec...]
where the time goes in v2:
time: 219 us
  Pallas kernels  117 us (53%)
  waiting for transfers between devices  55.9 us (26%)
  between operations  13.5 us (6%)
  local copies, waits for them, and re-layouts  11.7 us (5%)
  matrix products  11.7 us (5%)
  other arithmetic  9.06 us (4%)
    pallas_call x1, Pallas kernels, line_spectra(): pl.pallas_call(body, grid=(device_count * steps,), in_specs=[pl.BlockSpec...  117 us
    all_gather x1, waiting for transfers between devices, shards(): gathered = lax.all_gather(packed, ('rows', 'grp'), axis=0, tiled=False)  55.8 us
    dot_general x1, matrix products, row_transform(): jnp.einsum('eblk,ecbq->clqk', turned, second, precision=lax.Precision.HIGH)  6.09 us
    dot_general x1, matrix products, row_transform(): jnp.einsum('cubl,ceuk->eblk', grouped, first, precision=lax.Precision.HIGH)  5.56 us
    another operation x1, local copies, waits for them, and re-layouts, row_transform(): jnp.stack([turned[0] * tw_cos - turned[1] * tw_sin, turned[0] * tw_sin +...  5.51 us
    reshape x1, local copies, waits for them, and re-layouts, row_transform(): return image.reshape(2, lines, side)  4.94 us
  transfers between devices with their start and end apart: 1, of which 1 were waited for; matrix products, arithmetic and copies ran while one was open for 2% of the time, Pallas kernels for 0%

profile of v2, /device:TPU:0, one launch (start us, length us, event | category | flops | bytes accessed | tf_op | source)
XLA Modules:
  0.0 219.0 jit_solution(7972871941932041082)
XLA Ops:
  6.5 0.0 copy-start
  6.5 0.0 all-gather.4.cloned.1.call-start
  6.5 0.8 add_convert_fusion
  7.4 1.4 maximum_bitcast_fusion.4
  8.8 0.0 all-gather.4.cloned.1.call-update
  8.8 0.2 fusion.32
  9.0 0.1 reshape.260
  9.1 0.0 copy-done
  9.1 1.0 gather_fusion
  10.1 0.2 gather.8
  10.4 0.1 fusion.75
  10.5 0.1 fusion.71
  10.5 0.1 fusion.73
  10.6 0.3 fusion.58
  10.9 0.2 cosine_convert_fusion.1
  11.1 0.1 fusion.28
  11.2 0.3 fusion.54
  11.5 0.3 negate_convert_fusion
  11.9 0.1 fusion.18
  12.0 0.7 pad_maximum_fusion.1.table_ref
  12.7 0.6 fusion.46.taps_ref
  13.3 55.8 %all-gather.4.cloned.1.call-done.data_ref = f32[32,4,4096]{2,1,0:T(4,128)} async-done(((f32[1,4,4096]{2,1,0:T(4,128)}), f32[32,4,4096]{2,1,0:T(4,128)}) %all-gather.4.cloned.1.call-update) | async-done | bytes 2097168 | tf_op jit(solution)/shard_map/all_gather | solution.py:173
  69.2 117.2 %line_spectra.1 = f32[2,4096,128]{2,1,0:T(8,128)} custom-call(f32[32,4,4096]{2,1,0:T(4,128)} %all-gather.4.cloned.1.call-done.data_ref, f32[8,16,1]{2,1,0:T(8,128)} %fusion.46.taps_ref, bf16[384,224]{1,0:T(8,128)(2,1)} %pad_maximum_fusion.1.table_ref), custom_call_target="tpu_custom_call" | custom-call | tf_op jit(solution)/shard_map/line_spectra/pallas_call | solution.py:126
  186.4 5.6 %fusion.5 = f32[2,32,128,128]{2,3,1,0:T(8,128)S(1)} fusion(f32[2,128,32,128]{3,2,1,0:T(8,128)} %bitcast.49, f32[1,2,128,128]{2,3,0,1:T(8,128)S(1)} %get-tuple-element.8, f32[1,2,128,128]{2,3,0,1:T(8,128)S(1)} %get-tuple-element.7), kind=kOutput, calls=%fused_computation.7 | convolution fusion | flops 1610678272 | bytes 8650752 | tf_op jit(solution)/shard_map/cubl,ceuk->eblk/dot_general | solution.py:149
  192.0 1.4 multiply_subtract_fusion
  193.4 2.3 %pad_maximum_fusion = f32[2,32,128,128]{2,3,1,0:T(8,128)} fusion(f32[1,32,128,128]{2,3,1,0:T(8,128)S(1)} %get-tuple-element.6, f32[1,32,128,128]{2,3,1,0:T(8,128)S(1)} %get-tuple-element.5), kind=kLoop, calls=%fused_computation.1 | loop fusion | flops 1048576 | bytes 8388608 | tf_op jit(solution)/shard_map/stack | solution.py:153
  195.7 5.5 %copy.24 = f32[2,32,128,128]{3,1,0,2:T(8,128)} copy(f32[2,32,128,128]{2,3,1,0:T(8,128)} %pad_maximum_fusion) | data formatting | bytes 8388608 | tf_op jit(solution)/shard_map/stack | solution.py:153
  201.2 6.1 %fusion.8 = f32[2,128,32,128]{3,2,1,0:T(8,128)} fusion(f32[2,32,128,128]{3,1,0,2:T(8,128)} %copy.24, f32[1,2,32,32]{2,3,0,1:T(8,128)S(1)} %get-tuple-element.10, f32[1,2,32,32]{2,3,0,1:T(8,128)S(1)} %get-tuple-element.9), kind=kOutput, calls=%fused_computation.8 | convolution fusion | flops 402661376 | bytes 8404992 | tf_op jit(solution)/shard_map/eblk,ecbq->clqk/dot_general | solution.py:158
  207.2 4.9 %reshape.259 = f32[2,128,4096]{2,1,0:T(8,128)} reshape(f32[2,128,32,128]{3,2,1,0:T(8,128)} %fusion.8) | data formatting | bytes 8388608 | tf_op jit(solution)/shard_map/reshape | solution.py:161
  (5 shorter events, 0.0 us)
Async XLA Ops:
  6.5 2.6 %copy-start = (f32[8,8]{1,0:T(8,128)S(1)}, f32[8,8]{1,0:T(8,128)}, u32[]{:S(2)}) copy-start(f32[8,8]{1,0:T(8,128)} %param.7) | copy-start | bytes 772
  6.5 62.7 %all-gather.4.cloned.1.call-start = ((), (), s32[]{:S(2)}) async-start(), calls=%async_computation | async-start | bytes 2162688 | tf_op jit(solution)/shard_map/all_gather | solution.py:173
Sparse Core Ops, SparseCore 0:
  10.2 58.9 all-gather.3
